TPU v7x, 32 devices: a whole 2x2x4 slice. The times are simulated.
32 devices in a mesh: ens: 1, slab: 32 (over z, y, x, core).
Axes of the slice: x: 2, y: 2, z: 4, core: 2. Of those that a mesh axis runs over, the one named last changes fastest.
Arguments:
- field: bfloat16 [32, 256, 256, 128], P('ens', 'slab'), may hold values from -6 to 6
- w_x: bfloat16 [2, 32, 32, 32], replicated, may hold values from -0.75 to 0.75
- w_y: bfloat16 [2, 32, 32, 32], replicated, may hold values from -0.75 to 0.75
- w_z: bfloat16 [2, 32, 32, 32], replicated, may hold values from -0.75 to 0.75
- w_in: bfloat16 [32, 128], replicated, may hold values from -1 to 1
- b_in: float32 [128], replicated, may hold values from -3 to 3
- w_out: bfloat16 [128, 32], replicated, may hold values from -0.5 to 0.5
- b_out: float32 [32], replicated, may hold values from -2 to 2
Outputs:
- result: bfloat16 [32, 256, 256, 128], P('ens', 'slab')
All inputs are finite; a program needn't handle non-finite values.
Results may differ from a plain program's by a relative error of at most 0.0085.
Values may be sent and summed in bfloat16 or wider, within the bound.
A program may use at most 256 MiB of HBM per device.

v0:
```python
import math

import jax
import jax.numpy as jnp
from jax import lax
from jax.sharding import PartitionSpec as P


def tables(length, mode_count):
    position = jnp.arange(length, dtype=jnp.int32)
    frequency = jnp.arange(mode_count, dtype=jnp.int32)
    phase = position[:, None] * frequency[None, :] % length
    angles = phase.astype(jnp.float32) * (2.0 * math.pi / length)
    fwd_cos = jnp.cos(angles).astype(jnp.bfloat16)
    fwd_sin = (-jnp.sin(angles)).astype(jnp.bfloat16)
    factor = jnp.where(frequency == 0, 1.0, 2.0).astype(jnp.float32) / length
    inv_cos = (factor[:, None] * jnp.cos(angles).T).astype(jnp.bfloat16)
    inv_sin = (-factor[:, None] * jnp.sin(angles).T).astype(jnp.bfloat16)
    return (fwd_cos, fwd_sin, inv_cos, inv_sin)


def one_branch(field, weights, table_set, forward, mixing, inverse):
    fwd_cos, fwd_sin, inv_cos, inv_sin = table_set
    f32 = jnp.float32
    spec_re = jnp.einsum(forward, field, fwd_cos, preferred_element_type=f32).astype(jnp.bfloat16)
    spec_im = jnp.einsum(forward, field, fwd_sin, preferred_element_type=f32).astype(jnp.bfloat16)
    mixed_re = jnp.einsum(mixing, spec_re, weights[0], preferred_element_type=f32) - jnp.einsum(
        mixing, spec_im, weights[1], preferred_element_type=f32
    )
    mixed_im = jnp.einsum(mixing, spec_im, weights[0], preferred_element_type=f32) + jnp.einsum(
        mixing, spec_re, weights[1], preferred_element_type=f32
    )
    mixed_re = mixed_re.astype(jnp.bfloat16)
    mixed_im = mixed_im.astype(jnp.bfloat16)
    branch = jnp.einsum(inverse, mixed_re, inv_cos, preferred_element_type=f32)
    branch = branch + jnp.einsum(inverse, mixed_im, inv_sin, preferred_element_type=f32)
    return branch.astype(jnp.bfloat16)


def per_device(field, w_x, w_y, w_z, w_in, b_in, w_out, b_out):
    group_size = lax.axis_size("slab")
    len_x = field.shape[1] * group_size
    len_y = field.shape[2]
    len_z = field.shape[3]
    mode_count = w_x.shape[1]
    tables_x = tables(len_x, mode_count)
    tables_z = tables(len_z, mode_count)
    branch_y = one_branch(
        field, w_y, tables(len_y, mode_count), "cxyz,ym->cxmz", "cxmz,mcd->dxmz", "dxmz,my->dxyz"
    )
    line_x = one_branch(
        lax.all_to_all(field, "slab", split_axis=2, concat_axis=1, tiled=True),
        w_x,
        tables_x,
        "cxyz,xm->cmyz",
        "cmyz,mcd->dmyz",
        "dmyz,mx->dxyz",
    )
    branch_x = lax.all_to_all(line_x, "slab", split_axis=1, concat_axis=2, tiled=True)
    branch_z = one_branch(field, w_z, tables_z, "cxyz,zm->cmxy", "cmxy,mcd->dmxy", "dmxy,mz->dxyz")
    summed = (
        branch_x.astype(jnp.float32) + branch_y.astype(jnp.float32) + branch_z.astype(jnp.float32)
    ).astype(jnp.bfloat16)
    pre_act = (
        jnp.einsum("cxyz,ch->hxyz", summed, w_in, preferred_element_type=jnp.float32)
        + b_in[:, None, None, None]
    )
    hidden = jax.nn.gelu(pre_act, approximate=True).astype(jnp.bfloat16)
    output = (
        field.astype(jnp.float32)
        + jnp.einsum("hxyz,hc->cxyz", hidden, w_out, preferred_element_type=jnp.float32)
        + b_out[:, None, None, None]
    )
    return output.astype(jnp.bfloat16)


def solution(mesh):
    return jax.shard_map(
        per_device,
        mesh=mesh,
        in_specs=(P("ens", "slab", None, None), P(), P(), P(), P(), P(), P(), P()),
        out_specs=P("ens", "slab", None, None),
        check_vma=False,
    )
```

profile of v0, /device:TPU:0, one launch (start us, length us, event | category | flops | bytes accessed | tf_op | source)
XLA Modules:
  0.0 999.0 jit_solution(9221707674683376889)
XLA Ops:
  0.0 17.4 %copy.22 = bf16[32,8,256,128]{3,1,0,2:T(8,128)(2,1)} copy(bf16[32,8,256,128]{3,2,1,0:T(8,128)(2,1)} %param.8) | data formatting | bytes 33554432 | tf_op args[0]
  17.4 7.5 all-to-all-start
  24.9 372.6 %all-to-all-done = bf16[32,8,256,128]{3,1,0,2:T(8,128)(2,1)} async-done(((bf16[32,8,256,128]{3,1,0,2:T(8,128)(2,1)}), bf16[32,8,256,128]{3,1,0,2:T(8,128)(2,1)}, u32[]{:S(2)}, u32[]{:S(2)}) %all-to-all-start) | async-done | bytes 16777248 | tf_op jit(solution)/shard_map/all_to_all | solution.py:52
  397.5 10.3 %convert_bitcast_fusion.4 = bf16[32,32,8,128]{3,1,2,0:T(8,128)(2,1)S(1)} fusion(bf16[32,8,32,8,128]{4,1,0,3,2:T(8,128)(2,1)} %bitcast.4), kind=kOutput, calls=%fused_computation.57 | convolution fusion | flops 538050560 | bytes 18874368 | tf_op jit(solution)/shard_map/cxyz,xm->cmyz/dot_general | solution.py:26
  407.8 10.4 %convert_bitcast_fusion.5 = bf16[32,32,8,128]{3,1,2,0:T(8,128)(2,1)S(1)} fusion(bf16[32,8,32,8,128]{4,1,0,3,2:T(8,128)(2,1)} %bitcast.4), kind=kOutput, calls=%fused_computation.58 | convolution fusion | flops 538042368 | bytes 18874368 | tf_op jit(solution)/shard_map/cxyz,xm->cmyz/dot_general | solution.py:25
  429.9 13.3 %fusion.44 = f32[256,32,8,128]{3,0,2,1:T(8,128)} fusion(bf16[32,32,8,128]{3,0,2,1:T(8,128)(2,1)S(1)} %fusion.62, f32[32]{0:T(128)S(1)} %fusion.154), kind=kOutput, calls=%fused_computation.53 | convolution fusion | flops 537001984 | bytes 35651712 | tf_op jit(solution)/shard_map/dmyz,mx->dxyz/dot_general | solution.py:35
  443.2 12.9 %fusion.13 = bf16[32,256,8,128]{3,1,2,0:T(8,128)(2,1)S(1)} fusion(f32[256,32,8,128]{3,0,2,1:T(8,128)} %fusion.44, bf16[32,32,8,128]{3,0,2,1:T(8,128)(2,1)S(1)} %fusion.65, f32[32]{0:T(128)S(1)} %fusion.155), kind=kOutput, calls=%fused_computation.19 | convolution fusion | flops 553779200 | bytes 52428928 | tf_op jit(solution)/shard_map/dmyz,mx->dxyz/dot_general | solution.py:36
  456.1 36.9 %copy.32 = bf16[32,256,8,128]{3,2,0,1:T(8,128)(2,1)} copy(bf16[32,256,8,128]{3,1,2,0:T(8,128)(2,1)S(1)} %fusion.13) | data formatting | bytes 33554432 | tf_op jit(solution)/shard_map/convert_element_type | solution.py:37
  497.1 8.9 convert_bitcast_fusion.3
  508.7 8.9 convert_bitcast_fusion.2
  523.3 4.4 fusion.71
  527.7 13.7 %convert_bitcast_fusion = bf16[32,32,8,256]{3,1,2,0:T(8,128)(2,1)} fusion(bf16[32,8,256,128]{3,2,1,0:T(8,128)(2,1)} %param.8), kind=kOutput, calls=%fused_computation.35 | convolution fusion | flops 539033600 | bytes 20971520 | tf_op jit(solution)/shard_map/cxyz,zm->cmxy/dot_general | solution.py:26
  541.4 11.0 %fusion.28 = f32[32,8,256,32]{2,3,1,0:T(8,128)} fusion(bf16[32,32,8,256]{3,1,2,0:T(8,128)(2,1)} %convert_bitcast_fusion, bf16[2,32,32,32]{3,2,1,0:T(8,128)(2,1)S(1)} %copy-done.5), kind=kOutput, calls=%fused_computation.41 | convolution fusion | flops 134217728 | bytes 12845056 | tf_op jit(solution)/shard_map/cmxy,mcd->dmxy/dot_general | solution.py:27
  552.4 9.0 fusion.30
  561.5 13.6 %convert_bitcast_fusion.1 = bf16[32,32,8,256]{3,1,2,0:T(8,128)(2,1)} fusion(bf16[32,8,256,128]{3,2,1,0:T(8,128)(2,1)} %param.8), kind=kOutput, calls=%fused_computation.36 | convolution fusion | flops 539029504 | bytes 20971520 | tf_op jit(solution)/shard_map/cxyz,zm->cmxy/dot_general | solution.py:25
  575.1 10.6 %fusion.22 = bf16[32,32,8,256]{3,0,2,1:T(8,128)(2,1)S(1)} fusion(f32[32,8,256,32]{2,3,1,0:T(8,128)} %fusion.28, bf16[32,32,8,256]{3,1,2,0:T(8,128)(2,1)} %convert_bitcast_fusion.1, bf16[2,32,32,32]{3,2,1,0:T(8,128)(2,1)S(1)} %copy-done.5), kind=kOutput, calls=%fused_computation.29 | convolution fusion | flops 138412032 | bytes 17039360 | tf_op jit(solution)/shard_map/cmxy,mcd->dmxy/dot_general | solution.py:27
  585.7 5.9 fusion.23
  591.6 13.3 %fusion.41 = f32[256,32,8,128]{3,0,2,1:T(8,128)} fusion(bf16[32,8,32,128]{3,0,1,2:T(8,128)(2,1)S(1)} %fusion.68, f32[32]{0:T(128)S(1)} %fusion.154), kind=kOutput, calls=%fused_computation.50 | convolution fusion | flops 537001984 | bytes 35651712 | tf_op jit(solution)/shard_map/dxmz,my->dxyz/dot_general | solution.py:35
  604.9 13.7 %fusion.24 = f32[32,8,256,128]{3,2,1,0:T(8,128)} fusion(bf16[32,32,8,256]{3,0,2,1:T(8,128)(2,1)S(1)} %fusion.23, f32[32]{0:T(128)S(1)} %fusion.156), kind=kOutput, calls=%fused_computation.31 | convolution fusion | flops 536936448 | bytes 37748864 | tf_op jit(solution)/shard_map/dmxy,mz->dxyz/dot_general | solution.py:36
  618.6 13.9 %fusion.26 = f32[32,8,256,128]{3,2,1,0:T(8,128)} fusion(bf16[32,32,8,256]{3,0,2,1:T(8,128)(2,1)S(1)} %fusion.22, f32[32]{0:T(128)S(1)} %fusion.153), kind=kOutput, calls=%fused_computation.33 | convolution fusion | flops 536936448 | bytes 37748864 | tf_op jit(solution)/shard_map/dmxy,mz->dxyz/dot_general | solution.py:35
  632.5 237.0 %all-to-all-done.1 = bf16[32,256,8,128]{3,2,0,1:T(8,128)(2,1)} async-done(((bf16[32,256,8,128]{3,2,0,1:T(8,128)(2,1)}), bf16[32,256,8,128]{3,2,0,1:T(8,128)(2,1)}, u32[]{:S(2)}, u32[]{:S(2)}) %all-to-all-start.1) | async-done | bytes 16777248 | tf_op jit(solution)/shard_map/all_to_all | solution.py:59
  869.6 44.0 %fusion.9 = bf16[32,8,256,128]{3,2,1,0:T(8,128)(2,1)} fusion(f32[256,32,8,128]{3,0,2,1:T(8,128)} %fusion.41, f32[32,8,256,128]{3,2,1,0:T(8,128)} %fusion.26, f32[32,8,256,128]{3,2,1,0:T(8,128)} %fusion.24, bf16[32,8,32,128]{3,0,1,2:T(8,128)(2,1)S(1)} %copy-done.4, f32[32]{0:T(128)S(1)} %fusion.155, bf16[32,32,8,8,128]{4,3,0,2,1:T(8,128)(2,1)} %bitcast.71), kind=kOutput, calls=%fused_computation.11 | convolution fusion | flops 620888064 | bytes 136315008 | tf_op jit(solution)/shard_map/dxmz,my->dxyz/dot_general | solution.py:36
  913.6 69.9 %fusion.11 = bf16[32,8,256,128]{3,0,2,1:T(8,128)(2,1)} fusion(f32[128]{0:T(128)S(1)} %copy-done.9, bf16[32,8,256,128]{3,2,1,0:T(8,128)(2,1)} %fusion.9, bf16[32,8,256,128]{3,2,1,0:T(8,128)(2,1)} %param.8, f32[32]{0:T(128)S(1)} %copy-done.10, bf16[128,32]{0,1:T(8,128)(2,1)S(1)} %copy-done, bf16[32,128]{1,0:T(8,128)(2,1)S(1)} %copy-done.8), kind=kOutput, calls=%fused_computation.14 | convolution fusion | flops 4664066048 | bytes 50348672 | tf_op jit(solution)/shard_map/hxyz,hc->cxyz/dot_general | solution.py:71
  983.4 15.2 %copy.54 = bf16[32,8,256,128]{3,2,1,0:T(8,128)(2,1)} copy(bf16[32,8,256,128]{3,0,2,1:T(8,128)(2,1)} %fusion.11) | data formatting | bytes 33554432 | tf_op jit(solution)/shard_map/convert_element_type | solution.py:74
  (34 shorter events, 24.2 us)
Async XLA Ops:
  0.0 913.6 %copy-start = (bf16[128,32]{0,1:T(8,128)(2,1)S(1)}, bf16[128,32]{0,1:T(8,128)(2,1)}, u32[]{:S(2)}) copy-start(bf16[128,32]{0,1:T(8,128)(2,1)} %param.14) | copy-start | bytes 24580
  17.4 380.1 %all-to-all-start = ((bf16[32,8,256,128]{3,1,0,2:T(8,128)(2,1)}), bf16[32,8,256,128]{3,1,0,2:T(8,128)(2,1)}, u32[]{:S(2)}, u32[]{:S(2)}) async-start(bf16[32,8,256,128]{3,1,0,2:T(8,128)(2,1)} %copy.22), calls=%async_computation | async-start | bytes 33554432 | tf_op jit(solution)/shard_map/all_to_all | solution.py:52
  407.8 10.4 %copy-start.6 = (bf16[2,32,32,32]{3,2,1,0:T(8,128)(2,1)S(1)}, bf16[2,32,32,32]{3,2,1,0:T(8,128)(2,1)}, u32[]{:S(2)}) copy-start(bf16[2,32,32,32]{3,2,1,0:T(8,128)(2,1)} %param.9) | copy-start | bytes 393220
  493.0 376.6 %all-to-all-start.1 = ((bf16[32,256,8,128]{3,2,0,1:T(8,128)(2,1)}), bf16[32,256,8,128]{3,2,0,1:T(8,128)(2,1)}, u32[]{:S(2)}, u32[]{:S(2)}) async-start(bf16[32,256,8,128]{3,2,0,1:T(8,128)(2,1)} %copy.32), calls=%async_computation.1 | async-start | bytes 33554432 | tf_op jit(solution)/shard_map/all_to_all | solution.py:59
  497.0 8.9 copy-start.7
  527.7 13.7 %copy-start.5 = (bf16[2,32,32,32]{3,2,1,0:T(8,128)(2,1)S(1)}, bf16[2,32,32,32]{3,2,1,0:T(8,128)(2,1)}, u32[]{:S(2)}) copy-start(bf16[2,32,32,32]{3,2,1,0:T(8,128)(2,1)} %param.11) | copy-start | bytes 393220
  541.4 11.0 %copy-start.1 = (bf16[32,32,8,256]{3,1,2,0:T(8,128)(2,1)S(1)}, bf16[32,32,8,256]{3,1,2,0:T(8,128)(2,1)}, u32[]{:S(2)}) copy-start(bf16[32,32,8,256]{3,1,2,0:T(8,128)(2,1)} %convert_bitcast_fusion) | copy-start | bytes 12582916
  575.1 10.6 %copy-start.2 = (bf16[32,32,8,256]{3,1,2,0:T(8,128)(2,1)S(1)}, bf16[32,32,8,256]{3,1,2,0:T(8,128)(2,1)}, u32[]{:S(2)}) copy-start(bf16[32,32,8,256]{3,1,2,0:T(8,128)(2,1)} %convert_bitcast_fusion.1) | copy-start | bytes 12582916
  575.1 10.6 %copy-start.3 = (f32[32,8,256,32]{2,3,1,0:T(8,128)S(1)}, f32[32,8,256,32]{2,3,1,0:T(8,128)}, u32[]{:S(2)}) copy-start(f32[32,8,256,32]{2,3,1,0:T(8,128)} %fusion.30) | copy-start | bytes 25165828
  618.6 251.0 %copy-start.4 = (bf16[32,8,32,128]{3,0,1,2:T(8,128)(2,1)S(1)}, bf16[32,8,32,128]{3,0,1,2:T(8,128)(2,1)}, u32[]{:S(2)}) copy-start(bf16[32,8,32,128]{3,0,1,2:T(8,128)(2,1)} %fusion.71) | copy-start | bytes 6291460
  869.6 44.0 %copy-start.8 = (bf16[32,128]{1,0:T(8,128)(2,1)S(1)}, bf16[32,128]{1,0:T(8,128)(2,1)}, u32[]{:S(2)}) copy-start(bf16[32,128]{1,0:T(8,128)(2,1)} %param.12) | copy-start | bytes 24580
  869.6 44.0 %copy-start.9 = (f32[128]{0:T(128)S(1)}, f32[128]{0:T(128)}, u32[]{:S(2)}) copy-start(f32[128]{0:T(128)} %param.13) | copy-start | bytes 1540
  869.6 44.0 %copy-start.10 = (f32[32]{0:T(128)S(1)}, f32[32]{0:T(128)}, u32[]{:S(2)}) copy-start(f32[32]{0:T(128)} %param.15) | copy-start | bytes 388
where the time goes:
time: 1010 us; the launch traced here: 999 us
  waiting for transfers between devices  610 us (60%)
  matrix products  308 us (30%)
  local copies, waits for them, and re-layouts  69.5 us (7%)
  starting transfers between devices  11.5 us (1%)
    all_to_all x1, waiting for transfers between devices, per_device(): lax.all_to_all(field, 'slab', split_axis=2, concat_axis=1, tiled=True)  373 us
    all_to_all x1, waiting for transfers between devices, per_device(): lax.all_to_all(line_x, 'slab', split_axis=1, concat_axis=2, tiled=True)  237 us
    dot_general x3, matrix products, one_branch(): jnp.einsum(inverse, mixed_im, inv_sin, preferred_element_type=f32)  70.5 us
    dot_general x1, matrix products, per_device(): jnp.einsum('hxyz,hc->cxyz', hidden, w_out, preferred_element_type=jnp.flo...  69.9 us
    dot_general x3, matrix products, one_branch(): branch = jnp.einsum(inverse, mixed_re, inv_cos, preferred_element_type=f32)  40.5 us
    convert_element_type x1, local copies, waits for them, and re-layouts, one_branch(): return branch.astype(jnp.bfloat16)  36.9 us
    dot_general x3, matrix products, one_branch(): jnp.einsum(forward, field, fwd_cos, preferred_element_type=f32)  33 us
    dot_general x3, matrix products, one_branch(): jnp.einsum(forward, field, fwd_sin, preferred_element_type=f32)  32.9 us
  transfers between devices with their start and end apart: 2, of which 2 were waited for; matrix products, arithmetic and copies ran while one was open for 14% of the time, Pallas kernels for 0%

commit v1 on v0

v1 whole, which is shorter than its diff:
```python
import math

import jax
import jax.numpy as jnp
import numpy as np
from jax import lax
from jax.experimental.layout import Layout, with_layout_constraint
from jax.sharding import PartitionSpec as P

CHUNKS = 4


def tables(length, mode_count):
    phase = (np.arange(length)[:, None] * np.arange(mode_count)[None, :]) % length
    angles = phase.astype(np.float32) * np.float32(2.0 * math.pi / length)
    cos, sin = np.cos(angles), np.sin(angles)
    factor = (np.where(np.arange(mode_count) == 0, 1.0, 2.0) / length).astype(np.float32)
    fwd = np.stack([cos, -sin], axis=1)
    inv = np.stack([factor[:, None] * cos.T, -factor[:, None] * sin.T], axis=0)
    return jnp.asarray(fwd, jnp.bfloat16), jnp.asarray(inv, jnp.bfloat16)


def joint_weights(weights):
    re, im = weights[0], weights[1]
    from_re = jnp.stack([re, im], axis=2)
    from_im = jnp.stack([-im, re], axis=2)
    return jnp.stack([from_re, from_im], axis=1)


def mixed_modes(field, weights, fwd, forward, mixing):
    f32 = jnp.float32
    spec = jnp.einsum(forward, field, fwd, preferred_element_type=f32).astype(jnp.bfloat16)
    return jnp.einsum(mixing, spec, weights, preferred_element_type=f32).astype(jnp.bfloat16)


def inverse_of(mixed, inv, inverse):
    branch = jnp.einsum(inverse, mixed, inv, preferred_element_type=jnp.float32)
    return branch.astype(jnp.bfloat16)


def per_device(field, w_x, w_y, w_z, w_in, b_in, w_out, b_out):
    group_size = lax.axis_size("slab")
    len_x = field.shape[1] * group_size
    len_y = field.shape[2]
    len_z = field.shape[3]
    mode_count = w_x.shape[1]
    fwd_x, inv_x = tables(len_x, mode_count)
    fwd_y, inv_y = tables(len_y, mode_count)
    fwd_z, inv_z = tables(len_z, mode_count)
    joint_x, joint_y, joint_z = joint_weights(w_x), joint_weights(w_y), joint_weights(w_z)
    chunks = math.gcd(CHUNKS, len_y // group_size)
    rows = len_y // chunks
    f32 = jnp.float32

    channels, local_x = field.shape[0], field.shape[1]
    owned = rows // group_size
    fwd_x = fwd_x.reshape(group_size, local_x, 2, mode_count)
    inv_x = inv_x.reshape(2, mode_count, group_size, local_x)
    pieces = []
    branches_x = []
    for k in range(chunks):
        piece = lax.slice_in_dim(field, k * rows, (k + 1) * rows, axis=2)
        pieces.append(piece)
        sent = piece.reshape(channels, local_x, group_size, owned, len_z).transpose(2, 3, 0, 1, 4)
        sent = with_layout_constraint(sent, Layout((0, 3, 1, 2, 4)))
        line = lax.all_to_all(sent, "slab", split_axis=0, concat_axis=0, tiled=True)
        mixed = mixed_modes(line, joint_x, fwd_x, "nycxz,nxqm->qcmyz", "qcmyz,mqcpd->pdmyz")
        back = inverse_of(mixed, inv_x, "pdmyz,pmnx->nydxz")
        back = lax.all_to_all(back, "slab", split_axis=0, concat_axis=0, tiled=True)
        branches_x.append(back.transpose(2, 3, 0, 1, 4).reshape(piece.shape))

    mixed_y = mixed_modes(field, joint_y, fwd_y, "cxyz,yqm->qcxmz", "qcxmz,mqcpd->pdxmz")
    mixed_z = mixed_modes(field, joint_z, fwd_z, "cxyz,zqm->qcmxy", "qcmxy,mqcpd->pdmxy")
    result = jnp.zeros(field.shape, jnp.bfloat16)
    for k in range(chunks):
        y_part = inv_y[:, :, k * rows : (k + 1) * rows]
        z_part = lax.slice_in_dim(mixed_z, k * rows, (k + 1) * rows, axis=4)
        branch_y = inverse_of(mixed_y, y_part, "pdxmz,pmy->dxyz")
        branch_z = inverse_of(z_part, inv_z, "pdmxy,pmz->dxyz")
        summed = (
            branches_x[k].astype(f32) + branch_y.astype(f32) + branch_z.astype(f32)
        ).astype(jnp.bfloat16)
        pre_act = (
            jnp.einsum("cxyz,ch->hxyz", summed, w_in, preferred_element_type=f32)
            + b_in[:, None, None, None]
        )
        hidden = jax.nn.gelu(pre_act, approximate=True).astype(jnp.bfloat16)
        output = (
            pieces[k].astype(f32)
            + jnp.einsum("hxyz,hc->cxyz", hidden, w_out, preferred_element_type=f32)
            + b_out[:, None, None, None]
        )
        output = with_layout_constraint(output.astype(jnp.bfloat16), Layout((0, 1, 2, 3)))
        result = lax.dynamic_update_slice_in_dim(result, output, k * rows, axis=2)
    return result


def solution(mesh):
    return jax.shard_map(
        per_device,
        mesh=mesh,
        in_specs=(P("ens", "slab", None, None), P(), P(), P(), P(), P(), P(), P()),
        out_specs=P("ens", "slab", None, None),
        check_vma=False,
    )
```

time: 1010 us -> 945 us (0.936)
  matrix products: 308 us -> 207 us
  waiting for transfers between devices: 610 us -> 559 us
  other arithmetic: 0.02 us -> 50.9 us
  starting transfers between devices: 11.5 us -> 38.4 us
    dot_general x25 -> x28, matrix products: 308 us -> 207 us  [the longest x12 75.1 us: inverse_of(): branch = jnp.einsum(inverse, mixed, inv, preferred_element_type=jnp.float32)]
    all_to_all x2 -> x8, waiting for transfers between devices: 610 us -> 559 us  [the longest x4 334 us: per_device(): line = lax.all_to_all(sent, 'slab', split_axis=0, concat_axis=0, tiled=True)]
    convert_element_type x2 -> x4, local copies, waits for them, and re-layouts: 52 us -> 14.5 us  [inverse_of(): return branch.astype(jnp.bfloat16)]
    reshape x0 -> x4, local copies, waits for them, and re-layouts: none -> 34.1 us  [per_device(): piece.reshape(channels, local_x, group_size, owned, len_z)]
    all_to_all x2 -> x8, starting transfers between devices: 11.5 us -> 38.4 us  [the longest x4 20.6 us: per_device(): line = lax.all_to_all(sent, 'slab', split_axis=0, concat_axis=0, tiled=True)]
    convert_element_type x0 -> x5, other arithmetic: none -> 22.3 us  [the longest x4 14.8 us: per_device(): branches_x[k].astype(f32) + branch_y.astype(f32) + branch_z.astype(f32)]
    slice x0 -> x5, local copies, waits for them, and re-layouts: none -> 17.9 us  [the longest x1 11.8 us: per_device(): z_part = lax.slice_in_dim(mixed_z, k * rows, (k + 1) * rows, axis=4)]
    dynamic_update_slice x0 -> x2, other arithmetic: none -> 17.5 us  [per_device(): result = lax.dynamic_update_slice_in_dim(result, output, k * rows, axis=2)]
  transfers between devices with their start and end apart: 2 -> 8, of which waited for: 2 -> 8; matrix products, arithmetic and copies ran while one was open for 14% -> 20% of each run, Pallas kernels for 0% -> 0%
where the time goes in v1:
time: 945 us; the launch traced here: 936 us
  waiting for transfers between devices  559 us (59%)
  matrix products  207 us (22%)
  local copies, waits for them, and re-layouts  78.9 us (8%)
  other arithmetic  50.9 us (5%)
  starting transfers between devices  38.4 us (4%)
    all_to_all x4, waiting for transfers between devices, per_device(): line = lax.all_to_all(sent, 'slab', split_axis=0, concat_axis=0, tiled=True)  334 us
    all_to_all x4, waiting for transfers between devices, per_device(): back = lax.all_to_all(back, 'slab', split_axis=0, concat_axis=0, tiled=True)  226 us
    dot_general x12, matrix products, inverse_of(): branch = jnp.einsum(inverse, mixed, inv, preferred_element_type=jnp.float32)  75.1 us
    dot_general x4, matrix products, per_device(): jnp.einsum('hxyz,hc->cxyz', hidden, w_out, preferred_element_type=f32)  70.6 us
    dot_general x6, matrix products, mixed_modes(): jnp.einsum(forward, field, fwd, preferred_element_type=f32)  35.5 us
    reshape x4, local copies, waits for them, and re-layouts, per_device(): piece.reshape(channels, local_x, group_size, owned, len_z)  34.1 us
    dot_general x6, matrix products, mixed_modes(): jnp.einsum(mixing, spec, weights, preferred_element_type=f32)  26.1 us
    all_to_all x4, starting transfers between devices, per_device(): line = lax.all_to_all(sent, 'slab', split_axis=0, concat_axis=0, tiled=True)  20.6 us
  transfers between devices with their start and end apart: 8, of which 8 were waited for; matrix products, arithmetic and copies ran while one was open for 20% of the time, Pallas kernels for 0%

profile of v1, /device:TPU:0, one launch (start us, length us, event | category | flops | bytes accessed | tf_op | source)
XLA Modules:
  0.0 935.9 jit_solution(4061165210321320120)
XLA Ops:
  20.3 9.1 copy.318
  29.5 84.6 %all-to-all-done = bf16[32,2,32,8,128]{4,2,1,3,0:T(8,128)(2,1)} async-done(((bf16[32,2,32,8,128]{4,2,1,3,0:T(8,128)(2,1)}), bf16[32,2,32,8,128]{4,2,1,3,0:T(8,128)(2,1)}, u32[]{:S(2)}, u32[]{:S(2)}) %all-to-all-start) | async-done | bytes 4194336 | tf_op jit(solution)/shard_map/all_to_all | solution.py:66
  130.6 81.6 %all-to-all-done.2 = bf16[32,2,32,8,128]{4,2,1,3,0:T(8,128)(2,1)} async-done(((bf16[32,2,32,8,128]{4,2,1,3,0:T(8,128)(2,1)}), bf16[32,2,32,8,128]{4,2,1,3,0:T(8,128)(2,1)}, u32[]{:S(2)}, u32[]{:S(2)}) %all-to-all-start.2) | async-done | bytes 4194336 | tf_op jit(solution)/shard_map/all_to_all | solution.py:66
  227.6 83.0 %all-to-all-done.1 = bf16[32,2,32,8,128]{4,3,1,2,0:T(8,128)(2,1)} async-done(((bf16[32,2,32,8,128]{4,3,1,2,0:T(8,128)(2,1)}), bf16[32,2,32,8,128]{4,3,1,2,0:T(8,128)(2,1)}, u32[]{:S(2)}, u32[]{:S(2)}) %all-to-all-start.1) | async-done | bytes 4194336 | tf_op jit(solution)/shard_map/all_to_all | solution.py:69
  316.2 11.7 %convert_bitcast_fusion = bf16[2,32,32,8,256,1]{4,2,3,1,0,5:T(8,128)(2,1)} fusion(bf16[128,2,32,1,1]{0,2,4,3,1:T(8,128)(2,1)S(1)} %copy-done.25, bf16[32,8,256,128]{3,2,1,0:T(8,128)(2,1)} %param.14), kind=kOutput, calls=%fused_computation.83 | convolution fusion | flops 1077936128 | bytes 25182208 | tf_op jit(solution)/shard_map/cxyz,zqm->qcmxy/dot_general | solution.py:32
  327.9 17.6 %fusion.71 = bf16[2,32,32,8,256]{4,1,3,0,2:T(8,128)(2,1)} fusion(bf16[2,32,32,8,256,1]{4,2,3,1,0,5:T(8,128)(2,1)} %convert_bitcast_fusion, bf16[32,1,32,2,32]{2,4,1,3,0:T(8,128)(2,1)S(1)} %get-tuple-element.23, bf16[32,1,32,2,32]{2,4,1,3,0:T(8,128)(2,1)S(1)} %get-tuple-element.22), kind=kOutput, calls=%fused_computation.88 | convolution fusion | flops 541589504 | bytes 17039360 | tf_op jit(solution)/shard_map/qcmxy,mqcpd->pdmxy/dot_general | solution.py:33
  345.4 11.8 %fusion.188 = (bf16[2,32,32,8,64]{4,1,3,0,2:T(8,128)(2,1)}, bf16[2,32,32,8,64]{4,1,3,0,2:T(8,128)(2,1)}, bf16[2,32,32,8,64]{4,1,3,0,2:T(8,128)(2,1)}, bf16[2,32,32,8,64]{4,1,3,0,2:T(8,128)(2,1)S(1)}) fusion(bf16[2,32,32,8,256]{4,1,3,0,2:T(8,128)(2,1)} %fusion.71), kind=kLoop, calls=%fused_computation.204 | loop fusion | bytes 16777216 | tf_op jit(solution)/shard_map/slice | solution.py:77
  357.2 9.9 %fusion.90 = bf16[32,8,64,128,1]{3,2,4,1,0:T(8,128)(2,1)} fusion(bf16[2,32,128,1,1]{2,1,0,4,3:T(8,128)(2,1)S(1)} %copy-done.18, bf16[2,32,32,8,64]{4,1,3,0,2:T(8,128)(2,1)} %get-tuple-element.12), kind=kOutput, calls=%fused_computation.105 | convolution fusion | flops 268435456 | bytes 6307840 | tf_op jit(solution)/shard_map/pdmxy,pmz->dxyz/dot_general | solution.py:37
  387.8 9.6 %fusion.60 = bf16[32,8,64,128]{3,2,1,0:T(8,128)(2,1)} fusion(f32[32,8,64,128]{3,1,2,0:T(8,128)S(1)} %bitcast.410, bf16[32,8,64,128,1]{3,2,4,1,0:T(8,128)(2,1)S(1)} %copy-done.7, bf16[2,32,64,1,1]{2,1,0,4,3:T(8,128)(2,1)S(1)} %copy-done.24, bf16[2,32,8,32,128]{4,1,2,0,3:T(8,128)(2,1)S(1)} %fusion.75), kind=kOutput, calls=%fused_computation.79 | convolution fusion | flops 281018368 | bytes 20979712 | tf_op jit(solution)/shard_map/pdxmz,pmy->dxyz/dot_general | solution.py:37
  397.5 11.0 %all-to-all-done.3 = bf16[32,2,32,8,128]{4,3,1,2,0:T(8,128)(2,1)} async-done(((bf16[32,2,32,8,128]{4,3,1,2,0:T(8,128)(2,1)}), bf16[32,2,32,8,128]{4,3,1,2,0:T(8,128)(2,1)}, u32[]{:S(2)}, u32[]{:S(2)}) %all-to-all-start.3) | async-done | bytes 4194336 | tf_op jit(solution)/shard_map/all_to_all | solution.py:69
  413.2 9.8 %fusion.55 = bf16[32,8,64,128]{3,2,1,0:T(8,128)(2,1)} fusion(f32[32,8,64,128]{3,1,2,0:T(8,128)S(1)} %bitcast.411, bf16[32,8,64,128,1]{3,2,4,1,0:T(8,128)(2,1)S(1)} %copy-done.5, bf16[2,32,64,1,1]{2,1,0,4,3:T(8,128)(2,1)S(1)} %copy-done.23, bf16[2,32,8,32,128]{4,1,2,0,3:T(8,128)(2,1)S(1)} %copy-done.2), kind=kOutput, calls=%fused_computation.69 | convolution fusion | flops 281018368 | bytes 20979712 | tf_op jit(solution)/shard_map/pdxmz,pmy->dxyz/dot_general | solution.py:37
  423.0 17.6 %fusion.42 = f32[8,64,128,32]{2,3,1,0:T(8,128)} fusion(f32[128]{0:T(128)S(1)} %copy-done.28, bf16[32,8,64,128]{3,2,1,0:T(8,128)(2,1)} %fusion.60, bf16[128,32]{0,1:T(8,128)(2,1)S(1)} %copy-done, bf16[32,128]{1,0:T(8,128)(2,1)S(1)} %copy-done.27), kind=kOutput, calls=%fused_computation.44 | convolution fusion | flops 1157627904 | bytes 12599808 | tf_op jit(solution)/shard_map/hxyz,hc->cxyz/dot_general | solution.py:90
  440.7 17.8 %fusion.40 = f32[8,64,128,32]{2,3,1,0:T(8,128)} fusion(f32[128]{0:T(128)S(1)} %copy-done.28, bf16[32,8,64,128]{3,2,1,0:T(8,128)(2,1)} %fusion.55, bf16[128,32]{0,1:T(8,128)(2,1)S(1)} %copy-done, bf16[32,128]{1,0:T(8,128)(2,1)S(1)} %copy-done.27), kind=kOutput, calls=%fused_computation.43 | convolution fusion | flops 1157627904 | bytes 12599808 | tf_op jit(solution)/shard_map/hxyz,hc->cxyz/dot_general | solution.py:90
  474.1 10.3 %fusion.186 = (bf16[32,8,64,128]{3,2,1,0:T(8,128)(2,1)}, bf16[32,8,256,128]{3,2,1,0:T(8,128)(2,1)}, bf16[32,8,64,128]{3,2,1,0:T(8,128)(2,1)}) fusion(bf16[32,8,256,128]{3,2,1,0:T(8,128)(2,1)S(1)} %bitcast.408, bf16[32,8,256,128]{3,2,1,0:T(8,128)(2,1)} %dynamic_update_slice.12, f32[32]{0:T(128)S(1)} %copy-done.26, f32[8,64,128,32]{2,3,1,0:T(8,128)} %fusion.40), kind=kLoop, calls=%fused_computation.202 | loop fusion | flops 8388608 | bytes 33554560 | tf_op jit(solution)/shard_map/slice | solution.py:62
  484.5 9.1 copy.316
  497.9 9.0 copy.317
  507.0 84.6 %all-to-all-done.6 = bf16[32,2,32,8,128]{4,2,1,3,0:T(8,128)(2,1)} async-done(((bf16[32,2,32,8,128]{4,2,1,3,0:T(8,128)(2,1)}), bf16[32,2,32,8,128]{4,2,1,3,0:T(8,128)(2,1)}, u32[]{:S(2)}, u32[]{:S(2)}) %all-to-all-start.6) | async-done | bytes 4194336 | tf_op jit(solution)/shard_map/all_to_all | solution.py:66
  606.9 82.7 %all-to-all-done.4 = bf16[32,2,32,8,128]{4,2,1,3,0:T(8,128)(2,1)} async-done(((bf16[32,2,32,8,128]{4,2,1,3,0:T(8,128)(2,1)}), bf16[32,2,32,8,128]{4,2,1,3,0:T(8,128)(2,1)}, u32[]{:S(2)}, u32[]{:S(2)}) %all-to-all-start.4) | async-done | bytes 4194336 | tf_op jit(solution)/shard_map/all_to_all | solution.py:66
  705.0 82.9 %all-to-all-done.7 = bf16[32,2,32,8,128]{4,3,1,2,0:T(8,128)(2,1)} async-done(((bf16[32,2,32,8,128]{4,3,1,2,0:T(8,128)(2,1)}), bf16[32,2,32,8,128]{4,3,1,2,0:T(8,128)(2,1)}, u32[]{:S(2)}, u32[]{:S(2)}) %all-to-all-start.7) | async-done | bytes 4194336 | tf_op jit(solution)/shard_map/all_to_all | solution.py:69
  809.6 9.8 %fusion.47 = bf16[32,8,64,128]{3,2,1,0:T(8,128)(2,1)} fusion(f32[32,8,64,128]{3,1,2,0:T(8,128)S(1)} %bitcast.412, bf16[32,8,64,128,1]{3,2,4,1,0:T(8,128)(2,1)S(1)} %fusion.82, bf16[2,32,64,1,1]{2,1,0,4,3:T(8,128)(2,1)S(1)} %copy-done.22, bf16[2,32,8,32,128]{4,1,2,0,3:T(8,128)(2,1)S(1)} %copy-done.3), kind=kOutput, calls=%fused_computation.51 | convolution fusion | flops 281018368 | bytes 20979712 | tf_op jit(solution)/shard_map/pdxmz,pmy->dxyz/dot_general | solution.py:37
  819.4 17.6 %fusion.36 = f32[8,64,128,32]{2,3,1,0:T(8,128)} fusion(f32[128]{0:T(128)S(1)} %copy-done.28, bf16[32,8,64,128]{3,2,1,0:T(8,128)(2,1)} %fusion.47, bf16[128,32]{0,1:T(8,128)(2,1)S(1)} %copy-done, bf16[32,128]{1,0:T(8,128)(2,1)S(1)} %copy-done.27), kind=kOutput, calls=%fused_computation.41 | convolution fusion | flops 1157627904 | bytes 12599808 | tf_op jit(solution)/shard_map/hxyz,hc->cxyz/dot_general | solution.py:90
  837.0 48.9 %all-to-all-done.5 = bf16[32,2,32,8,128]{4,3,1,2,0:T(8,128)(2,1)} async-done(((bf16[32,2,32,8,128]{4,3,1,2,0:T(8,128)(2,1)}), bf16[32,2,32,8,128]{4,3,1,2,0:T(8,128)(2,1)}, u32[]{:S(2)}, u32[]{:S(2)}) %all-to-all-start.5) | async-done | bytes 4194336 | tf_op jit(solution)/shard_map/all_to_all | solution.py:69
  890.6 9.8 %fusion.51 = bf16[32,8,64,128]{3,2,1,0:T(8,128)(2,1)} fusion(f32[32,8,64,128]{3,1,2,0:T(8,128)S(1)} %bitcast.409, bf16[32,8,64,128,1]{3,2,4,1,0:T(8,128)(2,1)S(1)} %copy-done.6, bf16[2,32,64,1,1]{2,1,0,4,3:T(8,128)(2,1)S(1)} %copy-done.21, bf16[2,32,8,32,128]{4,1,2,0,3:T(8,128)(2,1)S(1)} %copy-done.4), kind=kOutput, calls=%fused_computation.60 | convolution fusion | flops 281018368 | bytes 20979712 | tf_op jit(solution)/shard_map/pdxmz,pmy->dxyz/dot_general | solution.py:37
  900.4 17.5 %fusion.38 = f32[8,64,128,32]{2,3,1,0:T(8,128)} fusion(f32[128]{0:T(128)S(1)} %copy-done.28, bf16[32,8,64,128]{3,2,1,0:T(8,128)(2,1)} %fusion.51, bf16[128,32]{0,1:T(8,128)(2,1)S(1)} %copy-done, bf16[32,128]{1,0:T(8,128)(2,1)S(1)} %copy-done.27), kind=kOutput, calls=%fused_computation.42 | convolution fusion | flops 1157627904 | bytes 12599808 | tf_op jit(solution)/shard_map/hxyz,hc->cxyz/dot_general | solution.py:90
  (134 shorter events, 177.4 us)
Async XLA Ops:
  0.0 423.0 %copy-start = (bf16[128,32]{0,1:T(8,128)(2,1)S(1)}, bf16[128,32]{0,1:T(8,128)(2,1)}, u32[]{:S(2)}) copy-start(bf16[128,32]{0,1:T(8,128)(2,1)} %param.20) | copy-start | bytes 24580
  12.9 101.2 %all-to-all-start = ((bf16[32,2,32,8,128]{4,2,1,3,0:T(8,128)(2,1)}), bf16[32,2,32,8,128]{4,2,1,3,0:T(8,128)(2,1)}, u32[]{:S(2)}, u32[]{:S(2)}) async-start(bf16[32,2,32,8,128]{4,2,1,3,0:T(8,128)(2,1)} %bitcast.417), calls=%async_computation | async-start | bytes 8388608 | tf_op jit(solution)/shard_map/all_to_all | solution.py:66
  114.0 98.1 %all-to-all-start.2 = ((bf16[32,2,32,8,128]{4,2,1,3,0:T(8,128)(2,1)}), bf16[32,2,32,8,128]{4,2,1,3,0:T(8,128)(2,1)}, u32[]{:S(2)}, u32[]{:S(2)}) async-start(bf16[32,2,32,8,128]{4,2,1,3,0:T(8,128)(2,1)} %bitcast.415), calls=%async_computation.2 | async-start | bytes 8388608 | tf_op jit(solution)/shard_map/all_to_all | solution.py:66
  119.4 102.4 %copy-start.11 = (bf16[32,1,32,2,32]{2,4,1,3,0:T(8,128)(2,1)}, bf16[32,1,32,2,32]{2,4,1,3,0:T(8,128)(2,1)S(1)}, u32[]{:S(2)}) copy-start(bf16[32,1,32,2,32]{2,4,1,3,0:T(8,128)(2,1)S(1)} %get-tuple-element.24) | copy-start | bytes 393220
  119.4 102.4 %copy-start.13 = (bf16[32,1,32,2,32]{2,4,1,3,0:T(8,128)(2,1)}, bf16[32,1,32,2,32]{2,4,1,3,0:T(8,128)(2,1)S(1)}, u32[]{:S(2)}) copy-start(bf16[32,1,32,2,32]{2,4,1,3,0:T(8,128)(2,1)S(1)} %get-tuple-element.25) | copy-start | bytes 393220
  212.2 98.3 %all-to-all-start.1 = ((bf16[32,2,32,8,128]{4,3,1,2,0:T(8,128)(2,1)}), bf16[32,2,32,8,128]{4,3,1,2,0:T(8,128)(2,1)}, u32[]{:S(2)}, u32[]{:S(2)}) async-start(bf16[32,2,32,8,128]{4,3,1,2,0:T(8,128)(2,1)} %copy.66), calls=%async_computation.1 | async-start | bytes 8388608 | tf_op jit(solution)/shard_map/all_to_all | solution.py:69
  227.5 87.2 %copy-start.16 = (bf16[2,32,32,32]{3,2,1,0:T(8,128)(2,1)S(1)}, bf16[2,32,32,32]{3,2,1,0:T(8,128)(2,1)}, u32[]{:S(2)}) copy-start(bf16[2,32,32,32]{3,2,1,0:T(8,128)(2,1)} %param.16) | copy-start | bytes 393220
  227.6 87.7 %copy-start.17 = (bf16[2,32,32,32]{3,2,1,0:T(8,128)(2,1)S(1)}, bf16[2,32,32,32]{3,2,1,0:T(8,128)(2,1)}, u32[]{:S(2)}) copy-start(bf16[2,32,32,32]{3,2,1,0:T(8,128)(2,1)} %param.17) | copy-start | bytes 393220
  310.5 98.0 %all-to-all-start.3 = ((bf16[32,2,32,8,128]{4,3,1,2,0:T(8,128)(2,1)}), bf16[32,2,32,8,128]{4,3,1,2,0:T(8,128)(2,1)}, u32[]{:S(2)}, u32[]{:S(2)}) async-start(bf16[32,2,32,8,128]{4,3,1,2,0:T(8,128)(2,1)} %copy.87), calls=%async_computation.3 | async-start | bytes 8388608 | tf_op jit(solution)/shard_map/all_to_all | solution.py:69
  345.4 11.8 %copy-start.18 = (bf16[2,32,128,1,1]{2,1,0,4,3:T(8,128)(2,1)S(1)}, bf16[2,32,128,1,1]{2,1,0,4,3:T(8,128)(2,1)}, u32[]{:S(2)}) copy-start(bf16[2,32,128,1,1]{2,1,0,4,3:T(8,128)(2,1)} %constant.44) | copy-start | bytes 49156
  345.4 28.5 %slice-start = ((s8[16777216]{0:T(1024)(128)(4,1)}), s8[4194304]{0:T(1024)(128)(4,1)S(1)}, s32[]{:S(2)}) async-start(s8[16777216]{0:T(1024)(128)(4,1)} %bitcast.405), calls=%async_computation.8 | async-start | bytes 8388608
  345.4 28.5 %slice-start.1 = ((s8[16777216]{0:T(1024)(128)(4,1)}), s8[4194304]{0:T(1024)(128)(4,1)S(1)}, s32[]{:S(2)}) async-start(s8[16777216]{0:T(1024)(128)(4,1)} %bitcast.405), calls=%async_computation.9 | async-start | bytes 8388608
  345.4 28.6 %slice-start.2 = ((s8[16777216]{0:T(1024)(128)(4,1)}), s8[4194304]{0:T(1024)(128)(4,1)S(1)}, s32[]{:S(2)}) async-start(s8[16777216]{0:T(1024)(128)(4,1)} %bitcast.405), calls=%async_computation.10 | async-start | bytes 8388608
  357.2 16.8 %slice-start.3 = ((s8[16777216]{0:T(1024)(128)(4,1)}), s8[4194304]{0:T(1024)(128)(4,1)S(1)}, s32[]{:S(2)}) async-start(s8[16777216]{0:T(1024)(128)(4,1)} %bitcast.405), calls=%async_computation.11 | async-start | bytes 8388608
  397.5 14.4 %copy-start.23 = (bf16[2,32,64,1,1]{2,1,0,4,3:T(8,128)(2,1)S(1)}, bf16[2,32,64,1,1]{2,1,0,4,3:T(8,128)(2,1)}, u32[]{:S(2)}) copy-start(bf16[2,32,64,1,1]{2,1,0,4,3:T(8,128)(2,1)} %constant.45) | copy-start | bytes 24580
  440.7 17.8 %copy-start.26 = (f32[32]{0:T(128)S(1)}, f32[32]{0:T(128)}, u32[]{:S(2)}) copy-start(f32[32]{0:T(128)} %param.21) | copy-start | bytes 388
  458.5 15.6 %slice-start.4 = ((s8[16777216]{0:T(1024)(128)(4,1)}), s8[4194304]{0:T(1024)(128)(4,1)S(1)}, s32[]{:S(2)}) async-start(s8[16777216]{0:T(1024)(128)(4,1)} %bitcast.407), calls=%async_computation.12 | async-start | bytes 8388608
  458.5 15.6 %slice-start.5 = ((s8[16777216]{0:T(1024)(128)(4,1)}), s8[4194304]{0:T(1024)(128)(4,1)S(1)}, s32[]{:S(2)}) async-start(s8[16777216]{0:T(1024)(128)(4,1)} %bitcast.407), calls=%async_computation.13 | async-start | bytes 8388608
  493.5 98.1 %all-to-all-start.6 = ((bf16[32,2,32,8,128]{4,2,1,3,0:T(8,128)(2,1)}), bf16[32,2,32,8,128]{4,2,1,3,0:T(8,128)(2,1)}, u32[]{:S(2)}, u32[]{:S(2)}) async-start(bf16[32,2,32,8,128]{4,2,1,3,0:T(8,128)(2,1)} %bitcast.418), calls=%async_computation.6 | async-start | bytes 8388608 | tf_op jit(solution)/shard_map/all_to_all | solution.py:66
  591.6 98.0 %all-to-all-start.4 = ((bf16[32,2,32,8,128]{4,2,1,3,0:T(8,128)(2,1)}), bf16[32,2,32,8,128]{4,2,1,3,0:T(8,128)(2,1)}, u32[]{:S(2)}, u32[]{:S(2)}) async-start(bf16[32,2,32,8,128]{4,2,1,3,0:T(8,128)(2,1)} %bitcast.416), calls=%async_computation.4 | async-start | bytes 8388608 | tf_op jit(solution)/shard_map/all_to_all | solution.py:66
  689.6 98.3 %all-to-all-start.7 = ((bf16[32,2,32,8,128]{4,3,1,2,0:T(8,128)(2,1)}), bf16[32,2,32,8,128]{4,3,1,2,0:T(8,128)(2,1)}, u32[]{:S(2)}, u32[]{:S(2)}) async-start(bf16[32,2,32,8,128]{4,3,1,2,0:T(8,128)(2,1)} %copy.113), calls=%async_computation.7 | async-start | bytes 8388608 | tf_op jit(solution)/shard_map/all_to_all | solution.py:69
  705.0 87.2 %copy-start.19 = (bf16[2,32,128,1,1]{2,1,0,4,3:T(8,128)(2,1)S(1)}, bf16[2,32,128,1,1]{2,1,0,4,3:T(8,128)(2,1)}, u32[]{:S(2)}) copy-start(bf16[2,32,128,1,1]{2,1,0,4,3:T(8,128)(2,1)} %constant.44) | copy-start | bytes 49156
  787.9 98.0 %all-to-all-start.5 = ((bf16[32,2,32,8,128]{4,3,1,2,0:T(8,128)(2,1)}), bf16[32,2,32,8,128]{4,3,1,2,0:T(8,128)(2,1)}, u32[]{:S(2)}, u32[]{:S(2)}) async-start(bf16[32,2,32,8,128]{4,3,1,2,0:T(8,128)(2,1)} %copy.100), calls=%async_computation.5 | async-start | bytes 8388608 | tf_op jit(solution)/shard_map/all_to_all | solution.py:69
  837.0 52.2 %copy-start.21 = (bf16[2,32,64,1,1]{2,1,0,4,3:T(8,128)(2,1)S(1)}, bf16[2,32,64,1,1]{2,1,0,4,3:T(8,128)(2,1)}, u32[]{:S(2)}) copy-start(bf16[2,32,64,1,1]{2,1,0,4,3:T(8,128)(2,1)} %constant.46) | copy-start | bytes 24580
  (23 other events, 121.1 us)
